TPU v7x, 32 devices: a whole 2x2x4 slice. The times are simulated.
32 devices in a mesh: group: 2 (over x), expert: 16 (over z, y, core).
Axes of the slice: x: 2, y: 2, z: 4, core: 2. Of those that a mesh axis runs over, the one named last changes fastest.
Arguments:
- query: bfloat16 [32, 2048], P(('group', 'expert')), parts along dimension 0, may hold values from -600 to 600
- key_new: bfloat16 [32, 2048], P(('group', 'expert')), parts along dimension 0, may hold values from -6 to 6
- value_new: bfloat16 [32, 2048], P(('group', 'expert')), parts along dimension 0, may hold values from -6 to 6
- key_cache: bfloat16 [32, 256, 2048], P(('group', 'expert')), parts along dimension 0, may hold values from -6 to 6
- value_cache: bfloat16 [32, 256, 2048], P(('group', 'expert')), parts along dimension 0, may hold values from -6 to 6
- lengths: int32 [32], P(('group', 'expert')), parts along dimension 0, may hold values from 1 to 256
- hidden: bfloat16 [32, 2048], P(('group', 'expert')), parts along dimension 0, may hold values from -6 to 6
- routes: int32 [32], P('group'), parts along dimension 0, may hold values from 0 to 31, as said below
- w_out: bfloat16 [2048, 2048], P(None, 'expert'), may hold values from -0.125 to 0.125
- ln_gain: bfloat16 [2048], replicated, may hold values from 0.099609375 to 1.8984375
- router: bfloat16 [2048, 32], replicated, may hold values from -0.125 to 0.125
- shared_up: bfloat16 [2048, 8192], P(None, 'expert'), may hold values from -0.125 to 0.125
- shared_down: bfloat16 [8192, 2048], P('expert'), may hold values from -0.0625 to 0.0625
- expert_up: bfloat16 [2048, 131072], P(None, 'expert'), may hold values from -0.125 to 0.125
- expert_down: bfloat16 [131072, 2048], P('expert'), may hold values from -0.09375 to 0.09375
Outputs:
- layer_out: bfloat16 [32, 2048], P(('group', 'expert')), parts along dimension 0
There are 2 independent parts, one for each index of `group`. A program takes and returns all parts, laid end to end along the dimension named above; an argument that names none is the same for every part. Nothing has to cross between parts.
Inputs may be any that keep to these rules, and one draw needn't show every extreme that they name: `routes`: no expert is named by more than 2 tokens of the group, and in every draw some expert is named by exactly 2.
All inputs are finite; a program needn't handle non-finite values.
Results may differ from a plain program's by a relative error of at most 0.0085.
Values may be sent and summed in bfloat16 or wider, within the bound.
A program may use at most 128 MiB of HBM per device.

v0:
```python
import math

import jax
import jax.numpy as jnp
from jax import lax
from jax.sharding import PartitionSpec as P

D = 2048
HEADS = 16
HEAD_DIM = 128
FF = 4096
EXPERTS = 32


def attend(query, key_new, value_new, key_cache, value_cache, lengths):
    seq_count = query.shape[0]
    cache_len = key_cache.shape[1]
    scale_factor = 1.0 / math.sqrt(HEAD_DIM)
    head_query = query.reshape(seq_count, HEADS, HEAD_DIM)
    head_keys = key_cache.reshape(seq_count, cache_len, HEADS, HEAD_DIM)
    head_values = value_cache.reshape(seq_count, cache_len, HEADS, HEAD_DIM)
    scores = (
        jnp.einsum("shd,schd->shc", head_query, head_keys, preferred_element_type=jnp.float32)
        * scale_factor
    )
    own_score = (
        jnp.einsum(
            "shd,shd->sh",
            head_query,
            key_new.reshape(seq_count, HEADS, HEAD_DIM),
            preferred_element_type=jnp.float32,
        )
        * scale_factor
    )
    positions = jnp.arange(cache_len, dtype=jnp.int32)
    scores = jnp.where(positions[None, None, :] < lengths[:, None, None], scores, -1e30)
    top_score = jnp.maximum(jnp.max(scores, axis=2), own_score)
    weights = jnp.exp(scores - top_score[:, :, None])
    own_weight = jnp.exp(own_score - top_score)
    normalizer = jnp.sum(weights, axis=2) + own_weight
    weights = (weights / normalizer[:, :, None]).astype(jnp.bfloat16)
    own_weight = (own_weight / normalizer).astype(jnp.bfloat16)
    mixed_values = jnp.einsum(
        "shc,schd->shd", weights, head_values, preferred_element_type=jnp.float32
    )
    mixed_values = mixed_values + own_weight.astype(jnp.float32)[:, :, None] * value_new.reshape(
        seq_count, HEADS, HEAD_DIM
    ).astype(jnp.float32)
    return mixed_values.reshape(seq_count, HEADS * HEAD_DIM).astype(jnp.bfloat16)


def body(
    query,
    key_new,
    value_new,
    key_cache,
    value_cache,
    lengths,
    hidden,
    routes,
    w_out,
    ln_gain,
    router,
    shared_up,
    shared_down,
    expert_up,
    expert_down,
):
    seq_count = query.shape[0]
    attended = attend(query, key_new, value_new, key_cache, value_cache, lengths)
    every_attended, every_hidden = (
        lax.all_gather(attended, "expert", axis=0, tiled=True),
        lax.all_gather(hidden, "expert", axis=0, tiled=True),
    )
    projected = jnp.dot(every_attended, w_out, preferred_element_type=jnp.float32).astype(
        jnp.bfloat16
    )
    every_projected = lax.all_gather(projected, "expert", axis=1, tiled=True)
    residual = every_hidden.astype(jnp.float32) + every_projected.astype(jnp.float32)
    centered = residual - jnp.mean(residual, axis=1, keepdims=True)
    variance = jnp.mean(centered * centered, axis=1, keepdims=True)
    normed = (
        centered / jnp.sqrt(jnp.maximum(variance, 0.25)) * ln_gain.astype(jnp.float32)
    ).astype(jnp.bfloat16)
    logits = jnp.dot(normed, router, preferred_element_type=jnp.float32)
    all_experts = jnp.arange(EXPERTS, dtype=jnp.int32)
    chosen = jnp.sum(jnp.where(routes[:, None] == all_experts[None, :], logits, 0.0), axis=1)
    gate_value = jax.nn.sigmoid(chosen)
    shared_hidden = jax.nn.gelu(
        jnp.dot(normed, shared_up, preferred_element_type=jnp.float32), approximate=True
    ).astype(jnp.bfloat16)
    total_tokens = routes.shape[0]
    capacity = 4 * total_tokens // EXPERTS
    column_count = expert_up.shape[1]
    local_units = min(column_count, FF)
    local_experts = column_count // local_units
    device_index = lax.axis_index("expert")
    first_expert = device_index * column_count // FF
    expert_ids = first_expert + jnp.arange(local_experts, dtype=jnp.int32)
    member = routes[:, None] == expert_ids[None, :]
    slot_rank = jnp.cumsum(member.astype(jnp.int32), axis=0) - 1
    slot_ids = jnp.arange(capacity, dtype=jnp.int32)
    placed = member[:, :, None] & (slot_rank[:, :, None] == slot_ids[None, None, :])
    picked = jnp.einsum(
        "skc,sd->kcd", placed.astype(jnp.bfloat16), normed, preferred_element_type=jnp.float32
    ).astype(jnp.bfloat16)
    up_local = expert_up.reshape(D, local_experts, local_units)
    inner_act = jax.nn.gelu(
        jnp.einsum("kcd,dkf->kcf", picked, up_local, preferred_element_type=jnp.float32),
        approximate=True,
    ).astype(jnp.bfloat16)
    down_local = expert_down.reshape(local_experts, local_units, D)
    result = jnp.einsum("kcf,kfd->kcd", inner_act, down_local, preferred_element_type=jnp.float32)
    spread = placed.astype(jnp.float32) * gate_value[:, None, None]
    summed = lax.psum_scatter(
        jnp.dot(shared_hidden, shared_down, preferred_element_type=jnp.float32)
        + jnp.einsum("skc,kcd->sd", spread, result, precision=lax.Precision.HIGHEST),
        "expert",
        scatter_dimension=0,
        tiled=True,
    )
    own_residual = lax.dynamic_slice_in_dim(residual, device_index * seq_count, seq_count, 0)
    combined = own_residual + summed
    return combined.astype(jnp.bfloat16)


def solution(mesh):
    placed = (
        P(("group", "expert"), None),
        P(("group", "expert"), None),
        P(("group", "expert"), None),
        P(("group", "expert"), None, None),
        P(("group", "expert"), None, None),
        P(("group", "expert")),
        P(("group", "expert"), None),
        P("group"),
        P(None, "expert"),
        P(),
        P(),
        P(None, "expert"),
        P("expert", None),
        P(None, "expert"),
        P("expert", None),
    )
    return jax.shard_map(
        body, mesh=mesh, in_specs=placed, out_specs=P(("group", "expert"), None), check_vma=False
    )
```

profile of v0, /device:TPU:0, one launch (start us, length us, event | category | flops | bytes accessed | tf_op | source)
XLA Modules:
  0.0 202.5 jit_solution(5360927554412156418)
XLA Ops:
  6.5 1.6 copy.43
  8.8 0.9 fusion.42
  9.8 0.7 reduce.5
  10.5 0.7 reduce.6
  11.2 0.1 fusion.39
  11.4 0.1 fusion.41
  11.5 0.2 fusion.38
  11.7 0.1 fusion.44
  11.8 1.5 copy.47
  13.2 0.7 convert_element_type.86
  13.9 0.3 fusion.4
  14.3 0.1 add_convert_fusion
  14.4 23.5 %all-gather.1 = bf16[16,1,2048]{2,1,0:T(2,128)(2,1)S(1)} all-gather(bf16[1,1,2048]{2,1,0:T(2,128)(2,1)S(1)} %reshape.187), channel_id=1, replica_groups=mesh['group'=2,'expert'=16] {'expert'}, dimensions={0}, use_global_device_ids=true | all-gather | bytes 69632 | tf_op jit(solution)/shard_map/all_gather | solution.py:72
  37.8 1.2 convolution_convert_fusion.1
  39.1 17.6 %all_gather.11 = bf16[16,2048]{1,0:T(8,128)(2,1)S(1)} all-gather(bf16[16,128]{1,0:T(8,128)(2,1)S(1)} %convolution_convert_fusion.1), channel_id=1, replica_groups=mesh['group'=2,'expert'=16] {'expert'}, dimensions={1}, use_global_device_ids=true | all-gather | bytes 69632 | tf_op jit(solution)/shard_map/all_gather | solution.py:78
  56.7 19.3 %all-gather = bf16[16,1,2048]{2,1,0:T(2,128)(2,1)S(1)} all-gather(bf16[1,1,2048]{2,1,0:T(2,128)(2,1)} %bitcast.69), channel_id=1, replica_groups=mesh['group'=2,'expert'=16] {'expert'}, dimensions={0}, use_global_device_ids=true | all-gather | bytes 69632 | tf_op jit(solution)/shard_map/all_gather | solution.py:73
  76.0 0.2 fusion.57
  76.2 0.2 multiply_reduce_fusion
  76.4 0.7 convert_element_type.79
  77.1 0.7 fusion.56
  77.9 0.1 copy.30
  77.9 0.1 copy.29
  78.0 0.1 multiply_convert_fusion
  78.1 1.2 fusion.3
  79.3 12.2 %fusion.15 = bf16[2,2,4096]{2,1,0:T(2,128)(2,1)S(1)} fusion(bf16[256,2,8,4096]{3,2,1,0:T(8,128)(2,1)} %bitcast.63, bf16[16,2048]{1,0:T(8,128)(2,1)S(1)} %multiply_convert_fusion, pred[16,2,2]{0,1,2:T(4,128)(4,1)S(1)} %compare_and_fusion), kind=kOutput, calls=%fused_computation.22 | convolution fusion | flops 67526656 | bytes 33652800 | tf_op jit(solution)/shard_map/kcd,dkf->kcf/dot_general | solution.py:109
  91.5 12.8 %fusion.60 = f32[2,2,2048]{2,1,0:T(2,128)S(1)} fusion(bf16[2,2,4096]{2,1,0:T(2,128)(2,1)S(1)} %fusion.15, bf16[2,4096,2048]{2,1,0:T(8,128)(2,1)} %bitcast.64), kind=kOutput, calls=%fused_computation.80 | convolution fusion | flops 67108864 | bytes 33619968 | tf_op jit(solution)/shard_map/kcf,kfd->kcd/dot_general | solution.py:113
  104.4 0.4 convolution_bitcast_fusion
  104.8 3.0 %convolution_add_fusion = f32[16,2048]{1,0:T(8,128)} fusion(f32[16,2048]{1,0:T(8,128)S(1)} %convolution_bitcast_fusion, bf16[512,2048]{1,0:T(8,128)(2,1)S(1)} %copy-done, bf16[16,2048]{1,0:T(8,128)(2,1)S(1)} %multiply_convert_fusion, bf16[2048,512]{1,0:T(8,128)(2,1)} %param.26), kind=kOutput, calls=%fused_computation.4 | convolution fusion | flops 67215360 | bytes 4521984 | tf_op jit(solution)/shard_map/dot_general | solution.py:116
  107.8 0.0 all-reduce.3.cloned.1.call-update
  107.8 0.6 dynamic-slice
  108.4 85.1 %all-reduce.3.cloned.1.call-done = f32[16,2048]{1,0:T(8,128)} async-done(((f32[16,2048]{1,0:T(8,128)}), f32[16,2048]{1,0:T(8,128)}) %all-reduce.3.cloned.1.call-update) | async-done | bytes 131088
  193.5 2.1 %fusion.40 = bf16[1,2048]{1,0:T(2,128)(2,1)} fusion(f32[16,2048]{1,0:T(8,128)} %all-reduce.3.cloned.1.call-done, u32[]{:T(128)} %bitcast.14, f32[16,2048]{1,0:T(8,128)S(1)} %get-tuple-element.6, s32[]{:T(128)S(6)} %select_n.18), kind=kLoop, calls=%fused_computation.48 | loop fusion | flops 4096 | bytes 20488 | tf_op jit(solution)/shard_map/convert_element_type | solution.py:124
  (16 shorter events, 0.1 us)
Async XLA Ops:
  6.5 98.2 %copy-start = (bf16[512,2048]{1,0:T(8,128)(2,1)S(1)}, bf16[512,2048]{1,0:T(8,128)(2,1)}, u32[]{:S(2)}) copy-start(bf16[512,2048]{1,0:T(8,128)(2,1)} %param.27) | copy-start | bytes 6291460
  6.5 187.0 %all-reduce.3.cloned.1.call-start = ((), (), s32[]{:S(2)}) async-start(), calls=%async_computation | async-start | bytes 262144
  91.5 16.3 %copy-start.1 = (u32[32]{0:T(128)S(1)}, u32[32]{0:T(128)}, u32[]{:S(2)}) copy-start(u32[32]{0:T(128)} %constant.69) | copy-start | bytes 388
Sparse Core Ops, SparseCore 0:
  107.9 85.5 all-reduce.2
where the time goes:
time: 204 us; the launch traced here: 202 us
  waiting for transfers between devices  85.1 us (42%)
  blocking collectives  60.4 us (30%)
  matrix products  32 us (16%)
  between operations  14.2 us (7%)
  other arithmetic  6.8 us (3%)
  local copies, waits for them, and re-layouts  3.92 us (2%)
    unnamed x2, waiting for transfers between devices  85.1 us
    all_gather x1, blocking collectives, body(): lax.all_gather(attended, 'expert', axis=0, tiled=True)  23.5 us
    all_gather x1, blocking collectives, body(): lax.all_gather(hidden, 'expert', axis=0, tiled=True)  19.3 us
    all_gather x1, blocking collectives, body(): every_projected = lax.all_gather(projected, 'expert', axis=1, tiled=True)  17.6 us
    dot_general x1, matrix products, body(): jnp.einsum('kcf,kfd->kcd', inner_act, down_local, preferred_element_type=...  12.8 us
    dot_general x1, matrix products, body(): jnp.einsum('kcd,dkf->kcf', picked, up_local, preferred_element_type=jnp.f...  12.2 us
  transfers between devices with their start and end apart: 1, of which 1 were waited for; matrix products, arithmetic and copies ran while one was open for 0% of the time, Pallas kernels for 0%

commit v1 on v0

v1 whole, which is shorter than its diff:
```python
import functools
import math

import jax
import jax.numpy as jnp
from jax import lax
from jax.experimental import pallas as pl
from jax.experimental.pallas import tpu as pltpu
from jax.sharding import PartitionSpec as P

HEADS = 16
HEAD_DIM = 128
FF = 4096
EXPERTS = 32
CHUNK = 512
BLOCK = 256
MAX_SLOTS = 26
EARLY = 4
GROUP_COLS = 1024
MESH = pl.DeviceIdType.MESH
F32 = jnp.float32
BF16 = jnp.bfloat16


def gelu(v):
    return 0.5 * v * (1.0 + jnp.tanh(math.sqrt(2.0 / math.pi) * (v + 0.044715 * (v * v * v))))


def kernel(
    n,
    slots,
    lengths_ref,
    routes_ref,
    query_hbm,
    key_new_hbm,
    value_new_hbm,
    hidden_hbm,
    gain_hbm,
    keys_hbm,
    values_hbm,
    w_out_hbm,
    router_hbm,
    shared_up_hbm,
    shared_down_hbm,
    up_hbm,
    down_hbm,
    out_ref,
    query,
    key_new,
    value_new,
    hidden,
    gain,
    keys,
    values,
    w_out,
    router,
    shared_up,
    shared_down,
    ring,
    attended_all,
    hidden_all,
    unfold,
    projected_all,
    inner,
    normed_ref,
    gate_ref,
    shared_ref,
    own_ref,
    send_buf,
    recv_buf,
    local_sem,
    ring_sem,
    send_sem,
    recv_sem,
):
    me = lax.axis_index("expert")
    width = query.shape[1]
    units = up_hbm.shape[1]
    up_chunks = units // CHUNK
    piece = min(units, width)
    pieces = units // piece
    per = min(CHUNK // BLOCK, pieces)
    chunks_per_block = pieces // per
    blocks = width // BLOCK
    total = up_chunks + blocks * chunks_per_block

    barrier = pltpu.get_barrier_semaphore()

    def greet(off, carry):
        pl.semaphore_signal(
            barrier, inc=1, device_id={"expert": lax.rem(me + off, n)}, device_id_type=MESH
        )
        return carry

    lax.fori_loop(1, n, greet, 0)

    local = [
        pltpu.make_async_copy(src, dst, local_sem.at[i])
        for i, (src, dst) in enumerate(
            [
                (query_hbm, query),
                (key_new_hbm, key_new),
                (keys_hbm, keys),
                (values_hbm, values),
                (value_new_hbm, value_new),
                (hidden_hbm, hidden),
                (w_out_hbm, w_out),
                (gain_hbm, gain),
                (router_hbm, router),
                (shared_up_hbm, shared_up),
                (shared_down_hbm, shared_down),
            ]
        )
    ]
    (
        query_copy,
        key_new_copy,
        keys_copy,
        values_copy,
        value_new_copy,
        hidden_copy,
        w_out_copy,
        gain_copy,
        router_copy,
        shared_up_copy,
        shared_down_copy,
    ) = local

    def up_copy(chunk, slot):
        return pltpu.make_async_copy(
            up_hbm.at[:, pl.ds(pl.multiple_of(chunk * CHUNK, CHUNK), CHUNK)],
            ring.at[slot],
            ring_sem.at[slot],
        )

    def start_down(chunk, slot):
        block = chunk // chunks_per_block
        part = chunk - block * chunks_per_block
        for p in range(per):
            pltpu.make_async_copy(
                down_hbm.at[
                    pl.ds(pl.multiple_of((part * per + p) * piece, piece), piece),
                    pl.ds(pl.multiple_of(block * BLOCK, BLOCK), BLOCK),
                ],
                ring.at[slot, pl.ds(0, piece), pl.ds(p * BLOCK, BLOCK)],
                ring_sem.at[slot],
            ).start()

    def wait_down(slot):
        landed = ring.at[slot, pl.ds(0, piece), pl.ds(0, per * BLOCK)]
        pltpu.make_async_copy(landed, landed, ring_sem.at[slot]).wait()

    for copy in local[:7]:
        copy.start()
    for chunk in range(min(EARLY, up_chunks)):
        up_copy(chunk, chunk).start()

    rows = lax.broadcasted_iota(jnp.int32, (HEADS, width), 0)
    lanes = lax.broadcasted_iota(jnp.int32, (HEADS, width), 1)
    own_lane = lanes // HEAD_DIM == rows

    def fold(x):
        row = lax.broadcasted_iota(jnp.int32, (HEADS, HEAD_DIM), 0)
        taken = jnp.zeros((HEADS, HEAD_DIM), F32)
        for h in range(HEADS):
            taken = taken + jnp.where(row == h, x[:, h * HEAD_DIM : (h + 1) * HEAD_DIM], 0.0)
        return taken

    scale = 1.0 / math.sqrt(HEAD_DIM)
    query_copy.wait()
    key_new_copy.wait()
    spread_query = jnp.where(
        own_lane, jnp.broadcast_to(query[...].astype(F32), (HEADS, width)), 0.0
    )
    own_score = (
        jnp.sum(spread_query * key_new[...].astype(F32), axis=1, keepdims=True) * scale
    )
    spread_query = spread_query.astype(BF16)
    keys_copy.wait()
    scores = (
        lax.dot_general(
            spread_query, keys[...], (((1,), (1,)), ((), ())), preferred_element_type=F32
        )
        * scale
    )
    values_copy.wait()
    value_new_copy.wait()
    hidden_copy.wait()
    w_out_copy.wait()
    for copy in local[7:]:
        copy.start()
    for chunk in range(EARLY, min(slots, up_chunks)):
        up_copy(chunk, chunk).start()
    for chunk in range(up_chunks, slots):
        start_down(chunk - up_chunks, chunk)

    position = lax.broadcasted_iota(jnp.int32, scores.shape, 1)
    scores = jnp.where(position < lengths_ref[0], scores, -1e30)
    top = jnp.maximum(jnp.max(scores, axis=1, keepdims=True), own_score)
    weights = jnp.exp(scores - top)
    own_weight = jnp.exp(own_score - top)
    normalizer = jnp.sum(weights, axis=1, keepdims=True) + own_weight
    weights = (weights / normalizer).astype(BF16)
    own_weight = (own_weight / normalizer).astype(BF16).astype(F32)
    mixed = jnp.dot(weights, values[...], preferred_element_type=F32)
    mixed = mixed + own_weight * value_new[...].astype(F32)
    mine = pl.ds(pl.multiple_of(me * HEADS, HEADS), HEADS)
    attended_all[mine, :] = fold(mixed).astype(BF16)
    hidden_all[mine, :] = fold(
        jnp.broadcast_to(hidden[...].astype(F32), (HEADS, width))
    ).astype(BF16)

    pl.semaphore_wait(barrier, n - 1)

    def send_all(src, dst, sem):
        def send(off, carry):
            pltpu.make_async_remote_copy(
                src_ref=src,
                dst_ref=dst,
                send_sem=send_sem.at[sem],
                recv_sem=recv_sem.at[sem],
                device_id={"expert": lax.rem(me + off, n)},
                device_id_type=MESH,
            ).start()
            return carry

        lax.fori_loop(1, n, send, 0)

    def await_bytes(ref, sem):
        pltpu.make_async_copy(ref, ref, sem).wait()

    send_all(attended_all.at[mine, :], attended_all.at[mine, :], 0)
    send_all(hidden_all.at[mine, :], hidden_all.at[mine, :], 1)

    others = pl.ds(0, (n - 1) * HEADS)
    await_bytes(attended_all.at[others, :], recv_sem.at[0])
    unfold[...] = attended_all[...].astype(F32)
    attended = jnp.concatenate(
        [unfold[pl.ds(h, n, stride=HEADS), :].astype(BF16) for h in range(HEADS)], axis=1
    )
    projected = jnp.dot(attended, w_out[...], preferred_element_type=F32).astype(BF16)
    cols = projected.shape[1]
    my_cols = pl.ds(pl.multiple_of(me * cols, cols), cols)
    if cols % 128 == 0:
        projected_all[:, my_cols] = projected
        piece_ref = projected_all.at[:, my_cols]
        arrived = projected_all.at[:, pl.ds(0, (n - 1) * cols)]
    else:
        projected_all[me] = projected
        piece_ref = projected_all.at[me]
        arrived = projected_all.at[pl.ds(0, n - 1)]
    send_all(piece_ref, piece_ref, 2)
    await_bytes(hidden_all.at[others, :], recv_sem.at[1])
    unfold[...] = hidden_all[...].astype(F32)
    every_hidden = jnp.concatenate(
        [unfold[pl.ds(h, n, stride=HEADS), :] for h in range(HEADS)], axis=1
    )
    token = lax.broadcasted_iota(jnp.int32, (n, 1), 0)
    chosen_expert = jnp.zeros((n, 1), jnp.int32)
    for t in range(n):
        chosen_expert = jnp.where(token == t, routes_ref[t], chosen_expert)
    gain_copy.wait()
    router_copy.wait()
    await_bytes(arrived, recv_sem.at[2])
    if cols % 128 == 0:
        every_projected = projected_all[...].astype(F32)
    else:
        every_projected = jnp.concatenate(
            [projected_all[d].astype(F32) for d in range(n)], axis=1
        )
    residual = every_hidden + every_projected
    centered = residual - jnp.mean(residual, axis=1, keepdims=True)
    variance = jnp.mean(centered * centered, axis=1, keepdims=True)
    normed = (
        centered / jnp.sqrt(jnp.maximum(variance, 0.25)) * gain[...].astype(F32).reshape(1, width)
    ).astype(BF16)
    normed_ref[...] = normed
    own_ref[...] = jnp.sum(jnp.where(token == me, residual, 0.0), axis=0, keepdims=True)

    shared_up_copy.wait()
    shared_ref[...] = gelu(
        jnp.dot(normed_ref[...], shared_up[...], preferred_element_type=F32)
    ).astype(BF16)
    logits = lax.dot_general(
        normed_ref[...], router[...], (((1,), (1,)), ((), ())), preferred_element_type=F32
    )
    expert_ids = lax.broadcasted_iota(jnp.int32, logits.shape, 1)
    chosen = jnp.sum(jnp.where(chosen_expert == expert_ids, logits, 0.0), axis=1, keepdims=True)
    gate_ref[...] = 1.0 / (1.0 + jnp.exp(-chosen))

    def up_step(chunk, carry):
        up_copy(chunk, chunk).wait()
        act = gelu(jnp.dot(normed_ref[...], ring[chunk], preferred_element_type=F32))
        expert = (me * units + chunk * CHUNK) // FF
        inner[:, pl.ds(pl.multiple_of(chunk * CHUNK, CHUNK), CHUNK)] = jnp.where(
            chosen_expert == expert, act, 0.0
        ).astype(BF16)

        @pl.when(chunk + slots < total)
        def _():
            start_down(chunk + slots - up_chunks, chunk)

        return carry

    lax.fori_loop(0, up_chunks, up_step, 0)
    shared_down_copy.wait()

    group_rows = GROUP_COLS // 128
    groups = width // GROUP_COLS
    blocks_per_group = blocks // groups
    slab = n * group_rows

    for group in range(groups):

        def down_step(index, carry, group=group):
            block = group * blocks_per_group + index
            acc = jnp.zeros((n, BLOCK), F32)
            for part in range(chunks_per_block):
                chunk = up_chunks + block * chunks_per_block + part
                slot = lax.rem(chunk, slots)
                wait_down(slot)
                for p in range(per):
                    acc = acc + jnp.dot(
                        inner[:, pl.ds((part * per + p) * piece, piece)],
                        ring[slot, pl.ds(0, piece), pl.ds(p * BLOCK, BLOCK)],
                        preferred_element_type=F32,
                    )
            shared = jnp.dot(
                shared_ref[...],
                shared_down[:, pl.ds(pl.multiple_of(block * BLOCK, BLOCK), BLOCK)],
                preferred_element_type=F32,
            )
            terms = shared + gate_ref[...] * acc
            for k in range(BLOCK // 128):
                row = group * slab + index * (BLOCK // 128) + k
                send_buf[pl.ds(row, n, stride=group_rows), :] = terms[:, k * 128 : (k + 1) * 128]
            return carry

        lax.fori_loop(0, blocks_per_group, down_step, 0)
        mine_slab = pl.ds(
            pl.multiple_of(group * slab + me * group_rows, group_rows), group_rows
        )

        def send_terms(off, carry, group=group, mine_slab=mine_slab):
            peer = lax.rem(me + off, n)
            pltpu.make_async_remote_copy(
                src_ref=send_buf.at[
                    pl.ds(pl.multiple_of(group * slab + peer * group_rows, group_rows), group_rows), :
                ],
                dst_ref=recv_buf.at[mine_slab, :],
                send_sem=send_sem.at[3 + group],
                recv_sem=recv_sem.at[3 + group],
                device_id={"expert": peer},
                device_id_type=MESH,
            ).start()
            return carry

        lax.fori_loop(1, n, send_terms, 0)
        recv_buf[mine_slab, :] = send_buf[mine_slab, :]

    for group in range(groups):
        landed = recv_buf.at[pl.ds(group * slab, (n - 1) * group_rows), :]
        await_bytes(landed, recv_sem.at[3 + group])
        summed = jnp.zeros((group_rows, 128), F32)
        for d in range(n):
            summed = summed + recv_buf[pl.ds(group * slab + d * group_rows, group_rows), :]
        for j in range(group_rows):
            where = pl.ds(group * GROUP_COLS + j * 128, 128)
            out_ref[:, where] = (own_ref[:, where] + summed[j : j + 1, :]).astype(out_ref.dtype)

    await_bytes(attended_all.at[others, :], send_sem.at[0])
    await_bytes(hidden_all.at[others, :], send_sem.at[1])
    await_bytes(arrived, send_sem.at[2])
    for group in range(groups):
        sent = send_buf.at[pl.ds(group * slab, (n - 1) * group_rows), :]
        await_bytes(sent, send_sem.at[3 + group])


def solution(mesh):
    n = mesh.shape["expert"]

    def body(
        query,
        key_new,
        value_new,
        key_cache,
        value_cache,
        lengths,
        hidden,
        routes,
        w_out,
        ln_gain,
        router,
        shared_up,
        shared_down,
        expert_up,
        expert_down,
    ):
        assert query.shape[0] == 1
        width = query.shape[1]
        units = expert_up.shape[1]
        cache = key_cache.shape[1]
        shared_units = shared_up.shape[1]
        cols = w_out.shape[1]
        piece = min(units, width)
        per = min(CHUNK // BLOCK, units // piece)
        total = units // CHUNK + (width // BLOCK) * (units // piece // per)
        slots = min(MAX_SLOTS, total)
        groups = width // GROUP_COLS
        flat = (width // GROUP_COLS) * n * (GROUP_COLS // 128)
        gathered = (n, width) if cols % 128 == 0 else (n, n, cols)
        vmem = pltpu.VMEM
        smem = pl.BlockSpec(memory_space=pltpu.SMEM)
        hbm = pl.BlockSpec(memory_space=pl.ANY)
        return pl.pallas_call(
            functools.partial(kernel, n, slots),
            out_shape=jax.ShapeDtypeStruct((1, width), BF16),
            in_specs=[smem] * 2 + [hbm] * 13,
            out_specs=pl.BlockSpec(memory_space=pltpu.VMEM),
            scratch_shapes=[
                vmem((1, width), BF16),
                vmem((1, width), BF16),
                vmem((1, width), BF16),
                vmem((1, width), BF16),
                vmem((width,), BF16),
                vmem((cache, width), BF16),
                vmem((cache, width), BF16),
                vmem((width, cols), BF16),
                vmem((EXPERTS, width), BF16),
                vmem((width, shared_units), BF16),
                vmem((shared_units, width), BF16),
                vmem((slots, width, CHUNK), BF16),
                vmem((n * HEADS, HEAD_DIM), BF16),
                vmem((n * HEADS, HEAD_DIM), BF16),
                vmem((n * HEADS, HEAD_DIM), F32),
                vmem(gathered, BF16),
                vmem((n, units), BF16),
                vmem((n, width), BF16),
                vmem((n, 1), F32),
                vmem((n, shared_units), BF16),
                vmem((1, width), F32),
                vmem((flat, 128), F32),
                vmem((flat, 128), F32),
                pltpu.SemaphoreType.DMA((11,)),
                pltpu.SemaphoreType.DMA((slots,)),
                pltpu.SemaphoreType.DMA((3 + groups,)),
                pltpu.SemaphoreType.DMA((3 + groups,)),
            ],
            compiler_params=pltpu.CompilerParams(
                collective_id=0, has_side_effects=True, vmem_limit_bytes=66_900_000
            ),
        )(
            lengths,
            routes,
            query,
            key_new,
            value_new,
            hidden,
            ln_gain,
            key_cache.reshape(cache, width),
            value_cache.reshape(cache, width),
            w_out,
            router.T,
            shared_up,
            shared_down,
            expert_up,
            expert_down,
        )

    rows = P(("group", "expert"), None)
    placed = (
        rows,
        rows,
        rows,
        P(("group", "expert"), None, None),
        P(("group", "expert"), None, None),
        P(("group", "expert")),
        rows,
        P("group"),
        P(None, "expert"),
        P(),
        P(),
        P(None, "expert"),
        P("expert", None),
        P(None, "expert"),
        P("expert", None),
    )
    return jax.shard_map(body, mesh=mesh, in_specs=placed, out_specs=rows, check_vma=False)
```

time: 204 us -> 48.1 us (0.24)
  waiting for transfers between devices: 85.1 us -> 0 us
  blocking collectives: 60.4 us -> 0 us
  Pallas kernels: 0 us -> 45.9 us
  matrix products: 32 us -> 0 us
  between operations: 14.2 us -> 0.66 us
  other arithmetic: 6.8 us -> 0 us
  local copies, waits for them, and re-layouts: 3.92 us -> 1.3 us
    unnamed x2 -> x0, waiting for transfers between devices: 85.1 us -> none
    all_gather x3 -> x0, blocking collectives: 60.4 us -> none  [the longest x1 23.5 us: body(): lax.all_gather(attended, 'expert', axis=0, tiled=True)]
    pallas_call x0 -> x1, Pallas kernels: none -> 45.9 us  [body(): pl.pallas_call(functools.partial(kernel, n, slots), out_shape=jax.ShapeDt...]
    dot_general x8 -> x0, matrix products: 32 us -> none  [the longest x1 12.8 us: body(): jnp.einsum('kcf,kfd->kcd', inner_act, down_local, preferred_element_type=...]
    convert_element_type x8 -> x0, other arithmetic: 4.48 us -> none  [the longest x1 2.08 us: body(): return combined.astype(jnp.bfloat16)]
  transfers between devices with their start and end apart: 1 -> 0, of which waited for: 1 -> 0; matrix products, arithmetic and copies ran while one was open for 0% -> 0% of each run, Pallas kernels for 0% -> 0%
where the time goes in v1:
time: 48.1 us; the launch traced here: 47.9 us
  Pallas kernels  45.9 us (95%)
  local copies, waits for them, and re-layouts  1.3 us (3%)
  between operations  0.66 us (1%)
    pallas_call x1, Pallas kernels, body(): pl.pallas_call(functools.partial(kernel, n, slots), out_shape=jax.ShapeDt...  45.9 us
    unnamed x1, local copies, waits for them, and re-layouts  1.3 us

profile of v1, /device:TPU:0, one launch (start us, length us, event | category | flops | bytes accessed | tf_op | source)
XLA Modules:
  0.0 47.9 jit_solution(12516831889107624039)
XLA Ops:
  0.7 45.9 %shard_map.145 = bf16[1,2048]{1,0:T(2,128)(2,1)} custom-call(s32[1]{0:T(128)S(6)} %copy.17.lengths_ref, s32[16]{0:T(128)} %routes_ref.1, bf16[1,2048]{1,0:T(2,128)(2,1)} %query_hbm.1, bf16[1,2048]{1,0:T(2,128)(2,1)} %key_new_hbm.1, bf16[1,2048]{1,0:T(2,128)(2,1)} %value_new_hbm.1, bf16[1,2048]{1,0:T(2,128)(2,1)} %hidden_hbm.1, bf16[2048]{0:T(1024)(128)(2,1)} %gain_hbm.1, ...), custom_call_target="tpu_custom_call" | custom-call | tf_op jit(solution)/shard_map/pallas_call | solution.py:415
  46.6 1.3 %copy.18 = bf16[1,2048]{1,0:T(2,128)(2,1)} copy(bf16[1,2048]{1,0:T(2,128)(2,1)} %shard_map.145) | data formatting | bytes 8192

commit v2 on v1

--- a/solution.py
+++ b/solution.py
@@ -13,9 +13,12 @@
 FF = 4096
 EXPERTS = 32
 CHUNK = 512
-BLOCK = 256
+BLOCK = 512
 MAX_SLOTS = 26
-EARLY = 4
+EARLY = 3
+PRIORITY = 1
+TOGETHER = 4
+JOINT = 1
 GROUP_COLS = 1024
 MESH = pl.DeviceIdType.MESH
 F32 = jnp.float32
@@ -79,20 +82,10 @@
     up_chunks = units // CHUNK
     piece = min(units, width)
     pieces = units // piece
-    per = min(CHUNK // BLOCK, pieces)
-    chunks_per_block = pieces // per
     blocks = width // BLOCK
-    total = up_chunks + blocks * chunks_per_block
+    total = up_chunks + blocks * pieces
 
     barrier = pltpu.get_barrier_semaphore()
-
-    def greet(off, carry):
-        pl.semaphore_signal(
-            barrier, inc=1, device_id={"expert": lax.rem(me + off, n)}, device_id_type=MESH
-        )
-        return carry
-
-    lax.fori_loop(1, n, greet, 0)
 
     local = [
         pltpu.make_async_copy(src, dst, local_sem.at[i])
@@ -133,27 +126,42 @@
             ring_sem.at[slot],
         )
 
-    def start_down(chunk, slot):
-        block = chunk // chunks_per_block
-        part = chunk - block * chunks_per_block
-        for p in range(per):
-            pltpu.make_async_copy(
-                down_hbm.at[
-                    pl.ds(pl.multiple_of((part * per + p) * piece, piece), piece),
-                    pl.ds(pl.multiple_of(block * BLOCK, BLOCK), BLOCK),
-                ],
-                ring.at[slot, pl.ds(0, piece), pl.ds(p * BLOCK, BLOCK)],
-                ring_sem.at[slot],
-            ).start()
-
-    def wait_down(slot):
-        landed = ring.at[slot, pl.ds(0, piece), pl.ds(0, per * BLOCK)]
-        pltpu.make_async_copy(landed, landed, ring_sem.at[slot]).wait()
-
-    for copy in local[:7]:
+    def down_copy(chunk, slot):
+        block = chunk // pieces
+        part = chunk - block * pieces
+        return pltpu.make_async_copy(
+            down_hbm.at[
+                pl.ds(pl.multiple_of(part * piece, piece), piece),
+                pl.ds(pl.multiple_of(block * BLOCK, BLOCK), BLOCK),
+            ],
+            ring.at[slot, pl.ds(0, piece), :],
+            ring_sem.at[slot],
+        )
+
+    def chunk_copy(chunk):
+        if chunk < up_chunks:
+            return up_copy(chunk, chunk)
+        return down_copy(chunk - up_chunks, chunk)
+
+    issued = 0
+
+    def start_chunks(last):
+        nonlocal issued
+        while issued < min(last, slots):
+            chunk_copy(issued).start(priority=PRIORITY)
+            issued += 1
+
+    for copy in (query_copy, key_new_copy, keys_copy, values_copy, value_new_copy, hidden_copy, w_out_copy):
         copy.start()
-    for chunk in range(min(EARLY, up_chunks)):
-        up_copy(chunk, chunk).start()
+    start_chunks(EARLY)
+
+    def greet(off, carry):
+        pl.semaphore_signal(
+            barrier, inc=1, device_id={"expert": lax.rem(me + off, n)}, device_id_type=MESH
+        )
+        return carry
+
+    lax.fori_loop(1, n, greet, 0)
 
     rows = lax.broadcasted_iota(jnp.int32, (HEADS, width), 0)
     lanes = lax.broadcasted_iota(jnp.int32, (HEADS, width), 1)
@@ -186,13 +194,9 @@
     values_copy.wait()
     value_new_copy.wait()
     hidden_copy.wait()
-    w_out_copy.wait()
     for copy in local[7:]:
         copy.start()
-    for chunk in range(EARLY, min(slots, up_chunks)):
-        up_copy(chunk, chunk).start()
-    for chunk in range(up_chunks, slots):
-        start_down(chunk - up_chunks, chunk)
+    start_chunks(slots)
 
     position = lax.broadcasted_iota(jnp.int32, scores.shape, 1)
     scores = jnp.where(position < lengths_ref[0], scores, -1e30)
@@ -238,6 +242,7 @@
     attended = jnp.concatenate(
         [unfold[pl.ds(h, n, stride=HEADS), :].astype(BF16) for h in range(HEADS)], axis=1
     )
+    w_out_copy.wait()
     projected = jnp.dot(attended, w_out[...], preferred_element_type=F32).astype(BF16)
     cols = projected.shape[1]
     my_cols = pl.ds(pl.multiple_of(me * cols, cols), cols)
@@ -288,21 +293,27 @@
     chosen = jnp.sum(jnp.where(chosen_expert == expert_ids, logits, 0.0), axis=1, keepdims=True)
     gate_ref[...] = 1.0 / (1.0 + jnp.exp(-chosen))
 
-    def up_step(chunk, carry):
-        up_copy(chunk, chunk).wait()
-        act = gelu(jnp.dot(normed_ref[...], ring[chunk], preferred_element_type=F32))
-        expert = (me * units + chunk * CHUNK) // FF
-        inner[:, pl.ds(pl.multiple_of(chunk * CHUNK, CHUNK), CHUNK)] = jnp.where(
-            chosen_expert == expert, act, 0.0
-        ).astype(BF16)
-
-        @pl.when(chunk + slots < total)
-        def _():
-            start_down(chunk + slots - up_chunks, chunk)
+    together = math.gcd(TOGETHER, up_chunks)
+
+    def up_step(step, carry):
+        chunks = [step * together + i for i in range(together)]
+        for chunk in chunks:
+            up_copy(chunk, chunk).wait()
+        for chunk in chunks:
+            act = gelu(jnp.dot(normed_ref[...], ring[chunk], preferred_element_type=F32))
+            expert = (me * units + chunk * CHUNK) // FF
+            inner[:, pl.ds(pl.multiple_of(chunk * CHUNK, CHUNK), CHUNK)] = jnp.where(
+                chosen_expert == expert, act, 0.0
+            ).astype(BF16)
+        for chunk in chunks:
+
+            @pl.when(chunk + slots < total)
+            def _(chunk=chunk):
+                down_copy(chunk + slots - up_chunks, chunk).start(priority=PRIORITY)
 
         return carry
 
-    lax.fori_loop(0, up_chunks, up_step, 0)
+    lax.fori_loop(0, up_chunks // together, up_step, 0)
     shared_down_copy.wait()
 
     group_rows = GROUP_COLS // 128
@@ -315,16 +326,17 @@
         def down_step(index, carry, group=group):
             block = group * blocks_per_group + index
             acc = jnp.zeros((n, BLOCK), F32)
-            for part in range(chunks_per_block):
-                chunk = up_chunks + block * chunks_per_block + part
-                slot = lax.rem(chunk, slots)
-                wait_down(slot)
-                for p in range(per):
-                    acc = acc + jnp.dot(
-                        inner[:, pl.ds((part * per + p) * piece, piece)],
-                        ring[slot, pl.ds(0, piece), pl.ds(p * BLOCK, BLOCK)],
-                        preferred_element_type=F32,
-                    )
+            first = up_chunks + block * pieces
+            held = [lax.rem(first + part, slots) for part in range(pieces)]
+            for part in range(pieces):
+                if part % JOINT == 0:
+                    for later in range(part, min(part + JOINT, pieces)):
+                        down_copy(first + later - up_chunks, held[later]).wait()
+                acc = acc + jnp.dot(
+                    inner[:, pl.ds(part * piece, piece)],
+                    ring[held[part], pl.ds(0, piece), :],
+                    preferred_element_type=F32,
+                )
             shared = jnp.dot(
                 shared_ref[...],
                 shared_down[:, pl.ds(pl.multiple_of(block * BLOCK, BLOCK), BLOCK)],
@@ -403,8 +415,7 @@
         shared_units = shared_up.shape[1]
         cols = w_out.shape[1]
         piece = min(units, width)
-        per = min(CHUNK // BLOCK, units // piece)
-        total = units // CHUNK + (width // BLOCK) * (units // piece // per)
+        total = units // CHUNK + (width // BLOCK) * (units // piece)
         slots = min(MAX_SLOTS, total)
         groups = width // GROUP_COLS
         flat = (width // GROUP_COLS) * n * (GROUP_COLS // 128)
@@ -414,7 +425,7 @@
         hbm = pl.BlockSpec(memory_space=pl.ANY)
         return pl.pallas_call(
             functools.partial(kernel, n, slots),
-            out_shape=jax.ShapeDtypeStruct((1, width), BF16),
+            out_shape=pltpu.VMEM((1, width), BF16),
             in_specs=[smem] * 2 + [hbm] * 13,
             out_specs=pl.BlockSpec(memory_space=pltpu.VMEM),
             scratch_shapes=[

time: 48.1 us -> 33.8 us (0.70)
  Pallas kernels: 45.9 us -> 32.3 us
  local copies, waits for them, and re-layouts: 1.3 us -> 0.6 us
    pallas_call x1, Pallas kernels: 45.9 us -> 32.3 us  [body(): pl.pallas_call(functools.partial(kernel, n, slots), out_shape=pltpu.VMEM(...]
    unnamed x1, local copies, waits for them, and re-layouts: 1.3 us -> 0.6 us
where the time goes in v2:
time: 33.8 us; the launch traced here: 33.6 us
  Pallas kernels  32.3 us (96%)
  between operations  0.66 us (2%)
  local copies, waits for them, and re-layouts  0.6 us (2%)
    pallas_call x1, Pallas kernels, body(): pl.pallas_call(functools.partial(kernel, n, slots), out_shape=pltpu.VMEM(...  32.3 us

profile of v2, /device:TPU:0, one launch (start us, length us, event | category | flops | bytes accessed | tf_op | source)
XLA Modules:
  0.0 33.6 jit_solution(2172892866763915213)
XLA Ops:
  0.7 32.3 %shard_map.145 = bf16[1,2048]{1,0:T(2,128)(2,1)S(1)} custom-call(s32[1]{0:T(128)S(6)} %copy.18.lengths_ref, s32[16]{0:T(128)} %routes_ref.1, bf16[1,2048]{1,0:T(2,128)(2,1)} %query_hbm.1, bf16[1,2048]{1,0:T(2,128)(2,1)} %key_new_hbm.1, bf16[1,2048]{1,0:T(2,128)(2,1)} %value_new_hbm.1, bf16[1,2048]{1,0:T(2,128)(2,1)} %hidden_hbm.1, bf16[2048]{0:T(1024)(128)(2,1)} %gain_hbm.1, ...), custom_call_target="tpu_custom_call" | custom-call | tf_op jit(solution)/shard_map/pallas_call | solution.py:426
  33.0 0.6 %copy.17 = bf16[1,2048]{1,0:T(2,128)(2,1)} copy(bf16[1,2048]{1,0:T(2,128)(2,1)S(1)} %shard_map.145) | data formatting | bytes 8192
